TPU v7x, 32 devices: a whole 2x2x4 slice. The times are simulated.
32 devices in a mesh: lat: 4 (over y, core), lon: 8 (over z, x).
Axes of the slice: x: 2, y: 2, z: 4, core: 2. Of those that a mesh axis runs over, the one named last changes fastest.
Arguments:
- forcing: float32 [640, 1024], P('lat', 'lon'), may hold values from -28 to 28
- search_direction: float32 [640, 1024], P('lat', 'lon'), may hold values from -28 to 28
- ocean_depth: float32 [640, 1024], P('lat', 'lon'), may hold values from 0.5 to 8
- land_mask: int32 [640, 1024], P('lat', 'lon'), may hold values 0 or 1
- fold_map: int32 [1024], replicated, may hold values from 0 to 1023, as said below
Outputs:
- scaled_height: float32 [640, 1024], P('lat', 'lon')
- residual: float32 [640, 1024], P('lat', 'lon')
Inputs may be any that keep to these rules, and one draw needn't show every extreme that they name: `fold_map`: column j's partner across the fold is (c - j) mod 1024 for one c of 0 to 1023, so the map is its own inverse.
All inputs are finite; a program needn't handle non-finite values. No bound on the sum of `land_mask` on one device may be relied on, other than what follows from the above.
Results may differ from a plain program's by a relative error of at most 0.0003.
Values sent between devices are 32-bit elements; how exact they have to be, the bound alone decides.
A program may use at most 64 MiB of HBM per device.

v0:
```python
import jax
import jax.numpy as jnp
import numpy as np
from jax import lax
from jax.sharding import PartitionSpec as P

STEPS = 8
REACH = 256
PRECISE = lax.Precision.HIGHEST
DIRECTIONS = ((1, 0), (-1, 0), (0, 1), (0, -1), (1, 1), (-1, -1), (1, -1), (-1, 1))
LINK_FACTORS = (1.0, 1.0, 1.0, 1.0, 0.5, 0.5, 0.5, 0.5)


def with_halo(x, sides, width):
    for axis, dim in sides:
        size, length = (lax.axis_size(axis), x.shape[dim])
        up = [(i, (i + 1) % size) for i in range(size)]
        down = [(j, i) for i, j in up]
        last = lax.slice_in_dim(x, length - width, length, axis=dim)
        leading = lax.slice_in_dim(x, 0, width, axis=dim)
        before = lax.ppermute(last, axis, up)
        after = lax.ppermute(leading, axis, down)
        x = jnp.concatenate([before, x, after], axis=dim)
    return x


def chebyshev_table(basis_steps):
    number = 2 * basis_steps + 1
    matrix = np.zeros((number, number), np.float32)
    for offset, length in ((0, basis_steps + 1), (basis_steps + 1, basis_steps)):
        for column in range(length - 1):
            matrix[offset + column, offset + column] = 1.0
            if column == 0:
                matrix[offset + 1, offset] = 1.0
            else:
                matrix[offset + column + 1, offset + column] = 0.5
                matrix[offset + column - 1, offset + column] = 0.5
    return matrix


def coordinates(gram_matrix, basis_steps):
    number = 2 * basis_steps + 1
    shift_matrix = jnp.asarray(chebyshev_table(basis_steps))
    unit_rows = jnp.eye(number, dtype=jnp.float32)
    solution_coords = jnp.zeros((number,), jnp.float32)
    direction_coords = unit_rows[0]
    residual_coords = unit_rows[basis_steps + 1]
    norm_now = jnp.dot(
        residual_coords, jnp.dot(gram_matrix, residual_coords, precision=PRECISE), precision=PRECISE
    )
    for inner_step in range(basis_steps):
        mapped = jnp.dot(shift_matrix, direction_coords, precision=PRECISE)
        curvature = jnp.dot(
            direction_coords, jnp.dot(gram_matrix, mapped, precision=PRECISE), precision=PRECISE
        )
        step_length = norm_now / curvature
        solution_coords = solution_coords + step_length * direction_coords
        residual_coords = residual_coords - step_length * mapped
        norm_next = jnp.dot(
            residual_coords,
            jnp.dot(gram_matrix, residual_coords, precision=PRECISE),
            precision=PRECISE,
        )
        direction_coords = residual_coords + norm_next / norm_now * direction_coords
        norm_now = norm_next
    return (solution_coords, residual_coords, direction_coords)


def trim_margin(source, margin_cells):
    if margin_cells == 0:
        return source
    return source[
        ...,
        margin_cells : source.shape[-2] - margin_cells,
        margin_cells : source.shape[-1] - margin_cells,
    ]


def place_fold(widened, fold_rows, fold_map, margin_cells):
    lat_count = lax.axis_size("lat")
    lat_place = lax.axis_index("lat")
    lon_width = widened.shape[-1] - 2 * margin_cells
    total_columns = fold_map.shape[0]
    columns = (
        lax.axis_index("lon") * lon_width
        - margin_cells
        + jnp.arange(lon_width + 2 * margin_cells, dtype=jnp.int32)
    ) % total_columns
    partners = jnp.take(fold_map, columns)
    mirrored = jnp.take(fold_rows[:, ::-1, :], partners, axis=2)
    north_rows = jnp.where(
        lat_place == lat_count - 1, mirrored, widened[:, widened.shape[1] - margin_cells :, :]
    )
    south_rows = jnp.where(lat_place == 0, 0.0, widened[:, :margin_cells, :])
    return jnp.concatenate(
        [south_rows, widened[:, margin_cells : widened.shape[1] - margin_cells, :], north_rows],
        axis=1,
    )


def extend_depth(fields, fold_map, margin_cells):
    widened = with_halo(fields, (("lat", 1), ("lon", 2)), margin_cells)
    fold_rows = lax.all_gather(
        fields[:, fields.shape[1] - margin_cells :, :], "lon", axis=2, tiled=True
    )
    return place_fold(widened, fold_rows, fold_map, margin_cells)


def extend_full(fields, fold_map, margin_cells):
    widened = with_halo(fields, (("lat", 1), ("lon", 2)), margin_cells)
    fold_rows = lax.all_gather(
        fields[:, fields.shape[1] - margin_cells :, :], "lon", axis=2, tiled=True
    )
    return place_fold(widened, fold_rows, fold_map, margin_cells)


def apply_power(source, source_depth, inverse_root, link_weights):
    outer_cut = STEPS - source_depth
    weighted = source * trim_margin(inverse_root, outer_cut)
    row_total = source.shape[-2] - 2
    column_total = source.shape[-1] - 2
    inner_weights = trim_margin(link_weights, outer_cut + 1)
    running = jnp.zeros((source.shape[0], row_total, column_total), jnp.float32)
    for direction_index in range(8):
        north_step, east_step = DIRECTIONS[direction_index]
        running = (
            running
            + inner_weights[direction_index]
            * weighted[
                :,
                1 + north_step : 1 + north_step + row_total,
                1 + east_step : 1 + east_step + column_total,
            ]
        )
    return -trim_margin(inverse_root, outer_cut + 1) * running


def advance(
    earlier, earlier_depth, current, current_depth, powers, stored, inverse_root, link_weights
):
    for power in powers:
        if power == STEPS - 1:
            earlier = earlier[:1]
            current = current[:1]
        upcoming = 2.0 * apply_power(
            current, current_depth, inverse_root, link_weights
        ) - trim_margin(earlier, earlier_depth - current_depth + 1)
        earlier, earlier_depth = (current, current_depth)
        current, current_depth = (upcoming, current_depth - 1)
        stored.append(trim_margin(current, current_depth))
    return (earlier, earlier_depth, current, current_depth)


def per_device(forcing, search_direction, ocean_depth, land_mask, fold_map):
    ocean_flag = land_mask.astype(jnp.float32)
    column_depth = ocean_depth * ocean_flag
    depth_wide = extend_depth(column_depth[None], fold_map, STEPS + 1)[0]
    wet_wide = (depth_wide > 0.0).astype(jnp.float32)
    centre_depth = trim_margin(depth_wide, 1)
    centre_wet = trim_margin(wet_wide, 1)
    row_total = depth_wide.shape[0] - 2
    column_total = depth_wide.shape[1] - 2
    weight_list = []
    link_sum = jnp.zeros_like(centre_depth)
    for direction_index in range(8):
        north_step, east_step = DIRECTIONS[direction_index]
        beside_depth = depth_wide[
            1 + north_step : 1 + north_step + row_total,
            1 + east_step : 1 + east_step + column_total,
        ]
        beside_wet = wet_wide[
            1 + north_step : 1 + north_step + row_total,
            1 + east_step : 1 + east_step + column_total,
        ]
        weight = (
            LINK_FACTORS[direction_index]
            * 0.5
            * (centre_depth + beside_depth)
            * centre_wet
            * beside_wet
        )
        weight_list.append(weight)
        link_sum = link_sum + weight
    link_weights = jnp.stack(weight_list)
    diagonal = centre_wet * (centre_depth / (REACH * REACH) + link_sum) + (1.0 - centre_wet)
    inverse_root = lax.rsqrt(diagonal)
    scaled_height = jnp.zeros_like(forcing)
    residual = ocean_flag * forcing
    direction = ocean_flag * search_direction
    chains = jnp.stack([direction, residual])
    earlier = extend_full(chains, fold_map, STEPS)
    earlier_depth = STEPS
    current = apply_power(earlier, earlier_depth, inverse_root, link_weights)
    current_depth = earlier_depth - 1
    stored = [trim_margin(earlier, earlier_depth), trim_margin(current, current_depth)]
    advance(
        earlier,
        earlier_depth,
        current,
        current_depth,
        range(1, STEPS),
        stored,
        inverse_root,
        link_weights,
    )
    krylov_basis = jnp.stack(
        [member[0] for member in stored] + [member[1] for member in stored[:STEPS]]
    )
    flattened = krylov_basis.reshape(krylov_basis.shape[0], -1)
    partial_gram = jnp.dot(flattened, flattened.T, precision=PRECISE)
    gram_matrix = lax.psum(partial_gram, ("lat", "lon"))
    solution_coords, residual_coords, direction_coords = coordinates(gram_matrix, STEPS)
    scaled_height = scaled_height + jnp.einsum(
        "k,kij->ij", solution_coords, krylov_basis, precision=PRECISE
    )
    residual = jnp.einsum("k,kij->ij", residual_coords, krylov_basis, precision=PRECISE)
    return (scaled_height, residual)


def solution(mesh):
    in_specs = (P("lat", "lon"), P("lat", "lon"), P("lat", "lon"), P("lat", "lon"), P())
    out_specs = (P("lat", "lon"), P("lat", "lon"))
    return jax.shard_map(
        per_device, mesh=mesh, in_specs=in_specs, out_specs=out_specs, check_vma=False
    )
```

profile of v0, /device:TPU:14, one launch (start us, length us, event | category | flops | bytes accessed | tf_op | source)
XLA Modules:
  0.0 225.7 jit_solution(7884336896558490846)
XLA Ops:
  0.7 1.0 copy.157
  1.7 1.0 copy.158
  2.6 1.0 copy.160
  3.6 1.0 copy.161
  5.4 1.7 collective-permute-start.1
  7.6 1.0 fusion.110
  8.6 1.7 collective-permute-start.5
  11.1 1.2 gather_fusion
  13.4 28.1 %all_gather.7 = f32[2,8,1024]{2,1,0:T(8,128)S(1)} all-gather(f32[2,8,128]{2,1,0:T(8,128)S(1)} %copy.165), channel_id=1, replica_groups=mesh['lat'=4,'lon'=8] {'lon'}, dimensions={2}, use_global_device_ids=true | all-gather | bytes 73728 | tf_op jit(solution)/shard_map/all_gather | solution.py:111
  41.5 1.2 gather_fusion.2
  44.5 31.5 %all_gather.6 = f32[1,9,1024]{1,2,0:T(8,128)S(1)} all-gather(f32[1,9,128]{1,2,0:T(8,128)} %get-tuple-element.75), channel_id=1, replica_groups=mesh['lat'=4,'lon'=8] {'lon'}, dimensions={2}, use_global_device_ids=true | all-gather | bytes 41472 | tf_op jit(solution)/shard_map/all_gather | solution.py:103
  77.3 2.3 %rev.7 = f32[2,8,1024]{1,0,2:T(2,128)S(1)} reverse(f32[2,8,1024]{1,0,2:T(2,128)S(1)} %copy.166), dimensions={1} | reverse | bytes 131072 | tf_op jit(solution)/shard_map/rev | solution.py:90
  79.6 0.8 gather_fusion.1
  80.4 0.9 gather_fusion.3
  81.5 2.0 collective-permute-start.3
  83.7 1.9 collective-permute-start.6
  85.6 1.2 collective-permute-start.7
  87.3 0.7 slice_select_fusion.3
  96.3 0.7 pad_maximum_fusion
  98.4 2.9 %broadcast_multiply_fusion.1 = (f32[2,174,142]{1,0,2:T(2,128)S(1)}, f32[2,174,142]{1,0,2:T(2,128)S(1)}) fusion(f32[174,142]{0,1:T(8,128)S(1)} %get-tuple-element.65, f32[2,176,144]{1,0,2:T(2,128)S(1)} %get-tuple-element.14, f32[174,142]{0,1:T(8,128)S(1)} %get-tuple-element.77, f32[174,142]{0,1:T(8,128)S(1)} %get-tuple-element.84, ...), kind=kLoop, calls=%fused_computation.244 | loop fusion | flops 840072 | bytes 2964960 | tf_op jit(solution)/shard_map/mul | solution.py:119
  101.3 1.2 fusion.197
  102.5 2.6 %broadcast_multiply_fusion.2 = (f32[2,172,140]{1,0,2:T(2,128)S(1)}, f32[2,172,140]{1,0,2:T(2,128)S(1)}) fusion(f32[172,140]{0,1:T(8,128)S(1)} %get-tuple-element.63, f32[2,176,144]{1,0,2:T(2,128)S(1)} %get-tuple-element.15, f32[2,174,142]{1,0,2:T(2,128)S(1)} %get-tuple-element.12, f32[172,140]{0,1:T(8,128)S(1)} %get-tuple-element.85, ...), kind=kLoop, calls=%fused_computation.245 | loop fusion | flops 915040 | bytes 3082240 | tf_op jit(solution)/shard_map/mul | solution.py:119
  105.2 2.6 %broadcast_multiply_fusion.3 = (f32[2,170,138]{1,0,2:T(2,128)S(1)}, f32[2,170,138]{1,0,2:T(2,128)S(1)}) fusion(f32[170,138]{0,1:T(8,128)S(1)} %get-tuple-element.61, f32[2,174,142]{1,0,2:T(2,128)S(1)} %get-tuple-element.13, f32[2,172,140]{1,0,2:T(2,128)S(1)} %get-tuple-element.10, f32[170,138]{0,1:T(8,128)S(1)} %get-tuple-element.93, ...), kind=kLoop, calls=%fused_computation.246 | loop fusion | flops 891480 | bytes 3002880 | tf_op jit(solution)/shard_map/mul | solution.py:119
  107.8 1.3 fusion.199
  109.1 1.3 fusion.198
  110.4 2.5 %broadcast_multiply_fusion.4 = (f32[2,168,136]{1,0,2:T(2,128)S(1)}, f32[2,168,136]{1,0,2:T(2,128)S(1)}) fusion(f32[168,136]{0,1:T(8,128)S(1)} %get-tuple-element.59, f32[2,172,140]{1,0,2:T(2,128)S(1)} %get-tuple-element.11, f32[2,170,138]{1,0,2:T(2,128)S(1)} %get-tuple-element.8, f32[168,136]{0,1:T(8,128)S(1)} %get-tuple-element.101, ...), kind=kLoop, calls=%fused_computation.279 | loop fusion | flops 868224 | bytes 2924544 | tf_op jit(solution)/shard_map/mul | solution.py:119
  113.0 2.6 %broadcast_multiply_fusion.5 = (f32[2,166,134]{1,0,2:T(2,128)S(1)}, f32[2,166,134]{1,0,2:T(2,128)S(1)}) fusion(f32[166,134]{0,1:T(8,128)S(1)} %get-tuple-element.57, f32[2,170,138]{1,0,2:T(2,128)S(1)} %get-tuple-element.9, f32[2,168,136]{1,0,2:T(2,128)S(1)} %get-tuple-element.6, f32[166,134]{0,1:T(8,128)S(1)} %get-tuple-element.109, ...), kind=kLoop, calls=%fused_computation.280 | loop fusion | flops 845272 | bytes 2847232 | tf_op jit(solution)/shard_map/mul | solution.py:119
  115.6 1.3 fusion.201
  116.9 1.3 fusion.200
  118.2 2.5 %broadcast_multiply_fusion.6 = (f32[2,164,132]{1,0,2:T(2,128)S(1)}, f32[2,164,132]{1,0,2:T(2,128)S(1)}) fusion(f32[164,132]{0,1:T(8,128)S(1)} %get-tuple-element.55, f32[2,168,136]{1,0,2:T(2,128)S(1)} %get-tuple-element.7, f32[2,166,134]{1,0,2:T(2,128)S(1)} %get-tuple-element.4, f32[164,132]{0,1:T(8,128)S(1)} %get-tuple-element.117, ...), kind=kLoop, calls=%fused_computation.281 | loop fusion | flops 822624 | bytes 2770944 | tf_op jit(solution)/shard_map/mul | solution.py:119
  120.7 2.6 %slice_subtract_fusion.5 = f32[2,162,130]{1,0,2:T(2,128)S(1)} fusion(f32[2,166,134]{1,0,2:T(2,128)S(1)} %get-tuple-element.5, f32[2,164,132]{1,0,2:T(2,128)S(1)} %get-tuple-element.2, f32[162,130]{0,1:T(8,128)S(1)} %get-tuple-element.125, f32[162,130]{0,1:T(8,128)S(1)} %get-tuple-element.132, f32[162,130]{0,1:T(8,128)S(1)} %get-tuple-element.126, ...), kind=kLoop, calls=%fused_computation.161 | loop fusion | flops 758160 | bytes 2442960 | tf_op jit(solution)/shard_map/sub | solution.py:145
  123.3 1.3 fusion.203
  124.8 1.2 fusion.204
  126.3 1.9 fusion.202
  128.2 7.4 %stack.48 = f32[17,160,128]{1,0,2:T(8,128)S(1)} concatenate(f32[1,160,128]{1,0,2:T(1,128)S(1)} %copy.178, f32[1,160,128]{1,0,2:T(1,128)} %get-tuple-element.32, f32[1,160,128]{1,0,2:T(1,128)} %get-tuple-element.34, f32[1,160,128]{1,0,2:T(1,128)} %get-tuple-element.36, f32[1,160,128]{1,0,2:T(1,128)} %get-tuple-element.38, f32[1,160,128]{1,0,2:T(1,128)} %get-tuple-element.40, ...), dimensions={0} | concatenate | bytes 2785280 | tf_op jit(solution)/shard_map/stack | solution.py:206
  135.6 3.4 %convolution_bitcast_fusion = f32[17,17]{1,0:T(8,128)S(1)} fusion(f32[17,160,128]{1,0,2:T(8,128)S(1)} %stack.48), kind=kOutput, calls=%fused_computation.4 | convolution fusion | flops 71024640 | bytes 1393796 | tf_op jit(solution)/shard_map/dot_general | solution.py:210
  139.0 46.3 %psum.7 = f32[17,17]{1,0:T(8,128)S(1)} all-reduce(f32[17,17]{1,0:T(8,128)S(1)} %convolution_bitcast_fusion), channel_id=1, replica_groups=mesh['lat'=4,'lon'=8] {'lat','lon'}, use_global_device_ids=true, to_apply=%region_0.1 | all-reduce | flops 289 | bytes 2312 | tf_op jit(solution)/shard_map/psum | solution.py:211
  188.8 0.7 fusion.18
  191.7 0.8 fusion.19
  196.0 0.8 fusion.21
  200.4 0.8 fusion.23
  204.7 0.8 fusion.25
  209.0 0.8 fusion.27
  213.4 0.8 fusion.29
  217.7 0.8 fusion.31
  219.8 1.7 fusion.131
  221.5 2.4 %fusion.133 = f32[1,160,128]{1,0,2:T(1,128)S(1)} fusion(f32[17,160,128]{1,0,2:T(8,128)S(1)} %stack.48, f32[17]{0:T(128)S(1)} %multiply_add_fusion, f32[17]{0:T(128)S(1)} %multiply_add_fusion.1, f32[17]{0:T(128)S(1)} %multiply_add_fusion.2, f32[17]{0:T(128)S(1)} %multiply_add_fusion.3, f32[17]{0:T(128)S(1)} %multiply_add_fusion.4, ...), kind=kOutput, calls=%fused_computation.364 | convolution fusion | flops 4178175 | bytes 1475580 | tf_op jit(solution)/shard_map/k,kij->ij/dot_general | solution.py:213
  224.0 0.7 copy.217
  (135 shorter events, 25.6 us)
Async XLA Ops:
  0.6 10.4 %copy-start = (s32[1024]{0:T(1024)S(1)}, s32[1024]{0:T(1024)}, u32[]{:S(2)}) copy-start(s32[1024]{0:T(1024)} %param.10) | copy-start | bytes 12292
  0.6 43.2 %copy-start.1 = (f32[17,17]{1,0:T(8,128)S(1)}, f32[17,17]{1,0:T(8,128)}, u32[]{:S(2)}) copy-start(f32[17,17]{1,0:T(8,128)} %constant.118.clone) | copy-start | bytes 3472
  5.4 76.0 %collective-permute-start = (f32[1,9,128]{1,2,0:T(8,128)}, f32[1,9,128]{1,2,0:T(8,128)S(1)}, u32[]{:S(2)}, u32[]{:S(2)}) collective-permute-start(f32[1,9,128]{1,2,0:T(8,128)} %get-tuple-element.75), channel_id=1, source_target_pairs={{0,8},{8,16},{16,24},{24,0},{1,9},{9,17},{17,25},{25,1},{2,10},{10... | collective-permute-start | bytes 13832 | tf_op jit(solution)/shard_map/ppermute | solution.py:21
  5.4 76.0 %collective-permute-start.1 = (f32[1,9,128]{1,2,0:T(8,128)}, f32[1,9,128]{1,2,0:T(8,128)S(1)}, u32[]{:S(2)}, u32[]{:S(2)}) collective-permute-start(f32[1,9,128]{1,2,0:T(8,128)} %get-tuple-element.76), channel_id=1, source_target_pairs={{8,0},{16,8},{24,16},{0,24},{9,1},{17,9},{25,17},{1,25},{10,2},{18... | collective-permute-start | bytes 13832 | tf_op jit(solution)/shard_map/ppermute | solution.py:22
  8.6 74.9 %collective-permute-start.4 = (f32[2,8,128]{1,0,2:T(2,128)S(1)}, f32[2,8,128]{1,0,2:T(2,128)S(1)}, u32[]{:S(2)}, u32[]{:S(2)}) collective-permute-start(f32[2,8,128]{1,0,2:T(2,128)S(1)} %get-tuple-element.46), channel_id=1, source_target_pairs={{0,8},{8,16},{16,24},{24,0},{1,9},{9,17},{17,25},{25,1},{2,10},{10... | collective-permute-start | bytes 24584 | tf_op jit(solution)/shard_map/ppermute | solution.py:21
  8.6 74.9 %collective-permute-start.5 = (f32[2,8,128]{1,0,2:T(2,128)}, f32[2,8,128]{1,0,2:T(2,128)S(1)}, u32[]{:S(2)}, u32[]{:S(2)}) collective-permute-start(f32[2,8,128]{1,0,2:T(2,128)} %get-tuple-element.47), channel_id=1, source_target_pairs={{8,0},{16,8},{24,16},{0,24},{9,1},{17,9},{25,17},{1,25},{10,2},{18... | collective-permute-start | bytes 24584 | tf_op jit(solution)/shard_map/ppermute | solution.py:22
  10.4 34.1 %copy-start.4 = (pred[17,17]{1,0:T(8,128)(4,1)}, pred[17,17]{1,0:T(8,128)(4,1)S(1)}, u32[]{:S(2)}) copy-start(pred[17,17]{1,0:T(8,128)(4,1)S(1)} %iota_compare_fusion) | copy-start | bytes 871
  81.4 5.4 %collective-permute-start.2 = (f32[1,178,9]{1,2,0:T(8,128)S(1)}, f32[1,178,9]{1,2,0:T(8,128)S(1)}, u32[]{:S(2)}, u32[]{:S(2)}) collective-permute-start(f32[1,178,9]{1,2,0:T(8,128)S(1)} %get-tuple-element.48), channel_id=1, source_target_pairs={{0,1},{1,2},{2,3},{3,4},{4,5},{5,6},{6,7},{7,0},{8,9},{9,10},{10,1... | collective-permute-start | bytes 19232 | tf_op jit(solution)/shard_map/ppermute | solution.py:21
  81.5 5.6 %collective-permute-start.3 = (f32[1,178,9]{1,2,0:T(8,128)S(1)}, f32[1,178,9]{1,2,0:T(8,128)S(1)}, u32[]{:S(2)}, u32[]{:S(2)}) collective-permute-start(f32[1,178,9]{1,2,0:T(8,128)S(1)} %get-tuple-element.49), channel_id=1, source_target_pairs={{1,0},{2,1},{3,2},{4,3},{5,4},{6,5},{7,6},{0,7},{9,8},{10,9},{11,1... | collective-permute-start | bytes 19232 | tf_op jit(solution)/shard_map/ppermute | solution.py:22
  83.5 5.2 %copy-start.2 = (f32[2,8,128]{1,0,2:T(2,128)}, f32[2,8,128]{1,0,2:T(2,128)S(1)}, u32[]{:S(2)}) copy-start(f32[2,8,128]{1,0,2:T(2,128)S(1)} %collective-permute-done.5) | copy-start | bytes 24580
  83.7 12.6 %collective-permute-start.6 = (f32[2,176,8]{1,0,2:T(2,128)S(1)}, f32[2,176,8]{1,0,2:T(2,128)S(1)}, u32[]{:S(2)}, u32[]{:S(2)}) collective-permute-start(f32[2,176,8]{1,0,2:T(2,128)S(1)} %get-tuple-element.27), channel_id=1, source_target_pairs={{0,1},{1,2},{2,3},{3,4},{4,5},{5,6},{6,7},{7,0},{8,9},{9,10},{10,1... | collective-permute-start | bytes 33800 | tf_op jit(solution)/shard_map/ppermute | solution.py:21
  85.6 10.6 %collective-permute-start.7 = (f32[2,176,8]{1,0,2:T(2,128)S(1)}, f32[2,176,8]{1,0,2:T(2,128)S(1)}, u32[]{:S(2)}, u32[]{:S(2)}) collective-permute-start(f32[2,176,8]{1,0,2:T(2,128)S(1)} %get-tuple-element.28), channel_id=1, source_target_pairs={{1,0},{2,1},{3,2},{4,3},{5,4},{6,5},{7,6},{0,7},{9,8},{10,9},{11,1... | collective-permute-start | bytes 33800 | tf_op jit(solution)/shard_map/ppermute | solution.py:22
  94.9 1.4 copy-start.3
  95.2 2.2 copy-start.7
  135.6 49.7 %copy-start.5 = (pred[17,17]{1,0:T(8,128)(4,1)S(1)}, pred[17,17]{1,0:T(8,128)(4,1)}, u32[]{:S(2)}) copy-start(pred[17,17]{1,0:T(8,128)(4,1)} %copy-done.4) | copy-start | bytes 871
  135.6 50.4 %copy-start.6 = (f32[1,17]{1,0:T(1,128)S(1)}, f32[1,17]{1,0:T(1,128)}, u32[]{:S(2)}) copy-start(f32[1,17]{1,0:T(1,128)} %fusion.123) | copy-start | bytes 208
where the time goes:
time: 230 us; the launch traced here: 226 us
  blocking collectives  106 us (46%)
  local copies, waits for them, and re-layouts  37.6 us (16%)
  other arithmetic  30.4 us (13%)
  between operations  21.8 us (9%)
  matrix products  21.1 us (9%)
  starting transfers between devices  8.72 us (4%)
    psum x1, blocking collectives, per_device(): gram_matrix = lax.psum(partial_gram, ('lat', 'lon'))  46.3 us
    all_gather x1, blocking collectives, extend_depth(): lax.all_gather(fields[:, fields.shape[1] - margin_cells:, :], 'lon', axis...  31.5 us
    all_gather x1, blocking collectives, extend_full(): lax.all_gather(fields[:, fields.shape[1] - margin_cells:, :], 'lon', axis...  28.1 us
    mul x8, other arithmetic, apply_power(): weighted = source * trim_margin(inverse_root, outer_cut)  16.5 us
    slice x6, local copies, waits for them, and re-layouts, per_device(): member[1]  7.88 us
    another operation x1, local copies, waits for them, and re-layouts, per_device(): jnp.stack([member[0] for member in stored] + [member[1] for member in sto...  7.44 us
    ppermute x4, starting transfers between devices, with_halo(): after = lax.ppermute(leading, axis, down)  6.73 us
    dot_general x8, matrix products, coordinates(): jnp.dot(gram_matrix, mapped, precision=PRECISE)  6.05 us
  transfers between devices with their start and end apart: 8, of which 1 were waited for; matrix products, arithmetic and copies ran while one was open for 10% of the time, Pallas kernels for 0%

commit v1 on v0

--- a/solution.py
+++ b/solution.py
@@ -208,7 +208,8 @@
     )
     flattened = krylov_basis.reshape(krylov_basis.shape[0], -1)
     partial_gram = jnp.dot(flattened, flattened.T, precision=PRECISE)
-    gram_matrix = lax.psum(partial_gram, ("lat", "lon"))
+    shards = lax.all_gather(partial_gram, ("lat", "lon"), axis=0, tiled=False)
+    gram_matrix = shards.sum(axis=0)
     solution_coords, residual_coords, direction_coords = coordinates(gram_matrix, STEPS)
     scaled_height = scaled_height + jnp.einsum(
         "k,kij->ij", solution_coords, krylov_basis, precision=PRECISE

time: 230 us -> 266 us (1.16)
  the two profiles are of different devices: /device:TPU:14 before, /device:TPU:0 now
where the time goes in v1:
time: 266 us; the launch traced here: 261 us
  blocking collectives  129 us (48%)
  local copies, waits for them, and re-layouts  38 us (14%)
  other arithmetic  30.3 us (11%)
  matrix products  27.6 us (10%)
  between operations  21.8 us (8%)
  starting transfers between devices  14 us (5%)
    all_gather x1, blocking collectives, per_device(): shards = lax.all_gather(partial_gram, ('lat', 'lon'), axis=0, tiled=False)  65.9 us
    all_gather x1, blocking collectives, extend_full(): lax.all_gather(fields[:, fields.shape[1] - margin_cells:, :], 'lon', axis...  31.7 us
    all_gather x1, blocking collectives, extend_depth(): lax.all_gather(fields[:, fields.shape[1] - margin_cells:, :], 'lon', axis...  31.4 us
    mul x8, other arithmetic, apply_power(): weighted = source * trim_margin(inverse_root, outer_cut)  16.5 us
    ppermute x4, starting transfers between devices, with_halo(): after = lax.ppermute(leading, axis, down)  11 us
    slice x6, local copies, waits for them, and re-layouts, per_device(): member[1]  7.92 us
    another operation x1, local copies, waits for them, and re-layouts, per_device(): jnp.stack([member[0] for member in stored] + [member[1] for member in sto...  7.44 us
    dot_general x8, matrix products, coordinates(): jnp.dot(gram_matrix, mapped, precision=PRECISE)  6.74 us
  transfers between devices with their start and end apart: 8, of which 0 were waited for; matrix products, arithmetic and copies ran while one was open for 8% of the time, Pallas kernels for 0%

profile of v1, /device:TPU:0, one launch (start us, length us, event | category | flops | bytes accessed | tf_op | source)
XLA Modules:
  0.0 260.7 jit_solution(1003614047794175117)
XLA Ops:
  0.7 1.0 copy.174
  1.7 1.0 copy.175
  2.6 1.0 copy.177
  3.6 1.0 copy.178
  5.9 1.9 collective-permute-start.1
  8.3 1.0 fusion.110
  10.0 1.1 collective-permute-start.5
  11.8 1.2 gather_fusion
  13.6 31.7 %all_gather.13 = f32[2,8,1024]{2,1,0:T(8,128)S(1)} all-gather(f32[2,8,128]{2,1,0:T(8,128)S(1)} %copy.182), channel_id=1, replica_groups=mesh['lat'=4,'lon'=8] {'lon'}, dimensions={2}, use_global_device_ids=true | all-gather | bytes 73728 | tf_op jit(solution)/shard_map/all_gather | solution.py:111
  45.2 1.2 gather_fusion.2
  47.2 31.4 %all_gather.12 = f32[1,9,1024]{1,2,0:T(8,128)S(1)} all-gather(f32[1,9,128]{1,2,0:T(8,128)} %get-tuple-element.75), channel_id=1, replica_groups=mesh['lat'=4,'lon'=8] {'lon'}, dimensions={2}, use_global_device_ids=true | all-gather | bytes 41472 | tf_op jit(solution)/shard_map/all_gather | solution.py:103
  79.8 2.4 rev.7
  82.9 1.5 gather_fusion.3
  84.3 0.8 pad_maximum_fusion.10
  85.1 1.8 collective-permute-start.2
  87.0 3.0 %collective-permute-start.3 = (f32[1,178,9]{1,2,0:T(8,128)S(1)}, f32[1,178,9]{1,2,0:T(8,128)S(1)}, u32[]{:S(2)}, u32[]{:S(2)}) collective-permute-start(f32[1,178,9]{1,2,0:T(8,128)S(1)} %get-tuple-element.49), channel_id=1, source_target_pairs={{1,0},{2,1},{3,2},{4,3},{5,4},{6,5},{7,6},{0,7},{9,8},{10,9},{11,1... | collective-permute-start | bytes 19232 | tf_op jit(solution)/shard_map/ppermute | solution.py:22
  90.2 5.0 %collective-permute-start.7 = (f32[2,176,8]{1,0,2:T(2,128)S(1)}, f32[2,176,8]{1,0,2:T(2,128)S(1)}, u32[]{:S(2)}, u32[]{:S(2)}) collective-permute-start(f32[2,176,8]{1,0,2:T(2,128)S(1)} %get-tuple-element.28), channel_id=1, source_target_pairs={{1,0},{2,1},{3,2},{4,3},{5,4},{6,5},{7,6},{0,7},{9,8},{10,9},{11,1... | collective-permute-start | bytes 33800 | tf_op jit(solution)/shard_map/ppermute | solution.py:22
  95.1 1.0 pad_maximum_fusion.2
  107.3 2.9 %broadcast_multiply_fusion.1 = (f32[2,174,142]{1,0,2:T(2,128)S(1)}, f32[2,174,142]{1,0,2:T(2,128)S(1)}) fusion(f32[174,142]{0,1:T(8,128)S(1)} %get-tuple-element.65, f32[2,176,144]{1,0,2:T(2,128)S(1)} %get-tuple-element.14, f32[174,142]{0,1:T(8,128)S(1)} %get-tuple-element.77, f32[174,142]{0,1:T(8,128)S(1)} %get-tuple-element.84, ...), kind=kLoop, calls=%fused_computation.244 | loop fusion | flops 840072 | bytes 2964960 | tf_op jit(solution)/shard_map/mul | solution.py:119
  110.2 1.2 fusion.197
  111.4 2.6 %broadcast_multiply_fusion.2 = (f32[2,172,140]{1,0,2:T(2,128)S(1)}, f32[2,172,140]{1,0,2:T(2,128)S(1)}) fusion(f32[172,140]{0,1:T(8,128)S(1)} %get-tuple-element.63, f32[2,176,144]{1,0,2:T(2,128)S(1)} %get-tuple-element.15, f32[2,174,142]{1,0,2:T(2,128)S(1)} %get-tuple-element.12, f32[172,140]{0,1:T(8,128)S(1)} %get-tuple-element.85, ...), kind=kLoop, calls=%fused_computation.245 | loop fusion | flops 915040 | bytes 3082240 | tf_op jit(solution)/shard_map/mul | solution.py:119
  114.0 2.6 %broadcast_multiply_fusion.3 = (f32[2,170,138]{1,0,2:T(2,128)S(1)}, f32[2,170,138]{1,0,2:T(2,128)S(1)}) fusion(f32[170,138]{0,1:T(8,128)S(1)} %get-tuple-element.61, f32[2,174,142]{1,0,2:T(2,128)S(1)} %get-tuple-element.13, f32[2,172,140]{1,0,2:T(2,128)S(1)} %get-tuple-element.10, f32[170,138]{0,1:T(8,128)S(1)} %get-tuple-element.93, ...), kind=kLoop, calls=%fused_computation.246 | loop fusion | flops 891480 | bytes 3002880 | tf_op jit(solution)/shard_map/mul | solution.py:119
  116.7 1.3 fusion.199
  118.0 1.3 fusion.198
  119.3 2.6 broadcast_multiply_fusion.4
  121.9 2.6 broadcast_multiply_fusion.5
  124.5 1.3 fusion.201
  125.8 1.3 fusion.200
  127.1 2.5 broadcast_multiply_fusion.6
  129.6 2.6 slice_subtract_fusion.5
  132.2 1.3 fusion.203
  133.7 1.2 fusion.204
  135.2 1.9 fusion.202
  137.1 7.4 %stack.48 = f32[17,160,128]{1,0,2:T(8,128)S(1)} concatenate(f32[1,160,128]{1,0,2:T(1,128)S(1)} %copy.195, f32[1,160,128]{1,0,2:T(1,128)} %get-tuple-element.32, f32[1,160,128]{1,0,2:T(1,128)} %get-tuple-element.34, f32[1,160,128]{1,0,2:T(1,128)} %get-tuple-element.36, f32[1,160,128]{1,0,2:T(1,128)} %get-tuple-element.38, f32[1,160,128]{1,0,2:T(1,128)} %get-tuple-element.40, ...), dimensions={0} | concatenate | bytes 2785280 | tf_op jit(solution)/shard_map/stack | solution.py:206
  144.6 3.4 %convolution_bitcast_fusion = f32[1,17,17]{2,1,0:T(8,128)S(1)} fusion(f32[17,160,128]{1,0,2:T(8,128)S(1)} %stack.48), kind=kOutput, calls=%fused_computation.4 | convolution fusion | flops 71024640 | bytes 1393796 | tf_op jit(solution)/shard_map/dot_general | solution.py:210
  147.9 65.9 %all-gather.1 = f32[32,17,17]{2,1,0:T(8,128)S(1)} all-gather(f32[1,17,17]{2,1,0:T(8,128)S(1)} %convolution_bitcast_fusion), channel_id=2, replica_groups=mesh['lat'=4,'lon'=8] {'lat','lon'}, dimensions={0}, use_global_device_ids=true | all-gather | bytes 38148 | tf_op jit(solution)/shard_map/all_gather | solution.py:211
  213.9 1.5 fusion.17
  215.3 1.4 fusion.16
  221.6 0.8 fusion.184
  226.6 0.8 fusion.182
  227.4 0.8 fusion.21
  231.6 0.8 fusion.180
  236.7 0.8 fusion.178
  241.7 0.8 fusion.176
  246.8 0.8 fusion.174
  251.8 0.8 fusion.172
  254.7 1.8 fusion.131
  256.5 2.4 fusion.133
  (132 shorter events, 30.4 us)
Async XLA Ops:
  0.6 11.1 %copy-start = (s32[1024]{0:T(1024)S(1)}, s32[1024]{0:T(1024)}, u32[]{:S(2)}) copy-start(s32[1024]{0:T(1024)} %param.10) | copy-start | bytes 12292
  0.6 45.8 %copy-start.1 = (f32[17,17]{1,0:T(8,128)S(1)}, f32[17,17]{1,0:T(8,128)}, u32[]{:S(2)}) copy-start(f32[17,17]{1,0:T(8,128)} %constant.118.clone) | copy-start | bytes 3472
  5.4 78.9 %collective-permute-start = (f32[1,9,128]{1,2,0:T(8,128)}, f32[1,9,128]{1,2,0:T(8,128)S(1)}, u32[]{:S(2)}, u32[]{:S(2)}) collective-permute-start(f32[1,9,128]{1,2,0:T(8,128)} %get-tuple-element.75), channel_id=1, source_target_pairs={{0,8},{8,16},{16,24},{24,0},{1,9},{9,17},{17,25},{25,1},{2,10},{10... | collective-permute-start | bytes 13832 | tf_op jit(solution)/shard_map/ppermute | solution.py:21
  5.9 78.5 %collective-permute-start.1 = (f32[1,9,128]{1,2,0:T(8,128)}, f32[1,9,128]{1,2,0:T(8,128)}, u32[]{:S(2)}, u32[]{:S(2)}) collective-permute-start(f32[1,9,128]{1,2,0:T(8,128)} %get-tuple-element.76), channel_id=1, source_target_pairs={{8,0},{16,8},{24,16},{0,24},{9,1},{17,9},{25,17},{1,25},{10,2},{18... | collective-permute-start | bytes 13832 | tf_op jit(solution)/shard_map/ppermute | solution.py:22
  9.3 80.6 %collective-permute-start.4 = (f32[2,8,128]{1,0,2:T(2,128)S(1)}, f32[2,8,128]{1,0,2:T(2,128)S(1)}, u32[]{:S(2)}, u32[]{:S(2)}) collective-permute-start(f32[2,8,128]{1,0,2:T(2,128)S(1)} %get-tuple-element.46), channel_id=1, source_target_pairs={{0,8},{8,16},{16,24},{24,0},{1,9},{9,17},{17,25},{25,1},{2,10},{10... | collective-permute-start | bytes 24584 | tf_op jit(solution)/shard_map/ppermute | solution.py:21
  10.0 79.9 %collective-permute-start.5 = (f32[2,8,128]{1,0,2:T(2,128)}, f32[2,8,128]{1,0,2:T(2,128)S(1)}, u32[]{:S(2)}, u32[]{:S(2)}) collective-permute-start(f32[2,8,128]{1,0,2:T(2,128)} %get-tuple-element.47), channel_id=1, source_target_pairs={{8,0},{16,8},{24,16},{0,24},{9,1},{17,9},{25,17},{1,25},{10,2},{18... | collective-permute-start | bytes 24584 | tf_op jit(solution)/shard_map/ppermute | solution.py:22
  11.1 35.4 %copy-start.5 = (pred[17,17]{1,0:T(8,128)(4,1)}, pred[17,17]{1,0:T(8,128)(4,1)S(1)}, u32[]{:S(2)}) copy-start(pred[17,17]{1,0:T(8,128)(4,1)S(1)} %iota_compare_fusion) | copy-start | bytes 871
  85.1 10.0 %collective-permute-start.2 = (f32[1,178,9]{1,2,0:T(8,128)S(1)}, f32[1,178,9]{1,2,0:T(8,128)S(1)}, u32[]{:S(2)}, u32[]{:S(2)}) collective-permute-start(f32[1,178,9]{1,2,0:T(8,128)S(1)} %get-tuple-element.48), channel_id=1, source_target_pairs={{0,1},{1,2},{2,3},{3,4},{4,5},{5,6},{6,7},{7,0},{8,9},{9,10},{10,1... | collective-permute-start | bytes 19232 | tf_op jit(solution)/shard_map/ppermute | solution.py:21
  87.0 8.2 %collective-permute-start.3 = (f32[1,178,9]{1,2,0:T(8,128)S(1)}, f32[1,178,9]{1,2,0:T(8,128)S(1)}, u32[]{:S(2)}, u32[]{:S(2)}) collective-permute-start(f32[1,178,9]{1,2,0:T(8,128)S(1)} %get-tuple-element.49), channel_id=1, source_target_pairs={{1,0},{2,1},{3,2},{4,3},{5,4},{6,5},{7,6},{0,7},{9,8},{10,9},{11,1... | collective-permute-start | bytes 19232 | tf_op jit(solution)/shard_map/ppermute | solution.py:22
  89.9 7.7 %copy-start.2 = (f32[2,8,128]{1,0,2:T(2,128)}, f32[2,8,128]{1,0,2:T(2,128)S(1)}, u32[]{:S(2)}) copy-start(f32[2,8,128]{1,0,2:T(2,128)S(1)} %collective-permute-done.5) | copy-start | bytes 24580
  90.1 15.0 %collective-permute-start.6 = (f32[2,176,8]{1,0,2:T(2,128)S(1)}, f32[2,176,8]{1,0,2:T(2,128)S(1)}, u32[]{:S(2)}, u32[]{:S(2)}) collective-permute-start(f32[2,176,8]{1,0,2:T(2,128)S(1)} %get-tuple-element.27), channel_id=1, source_target_pairs={{0,1},{1,2},{2,3},{3,4},{4,5},{5,6},{6,7},{7,0},{8,9},{9,10},{10,1... | collective-permute-start | bytes 33800 | tf_op jit(solution)/shard_map/ppermute | solution.py:21
  90.2 15.0 %collective-permute-start.7 = (f32[2,176,8]{1,0,2:T(2,128)S(1)}, f32[2,176,8]{1,0,2:T(2,128)S(1)}, u32[]{:S(2)}, u32[]{:S(2)}) collective-permute-start(f32[2,176,8]{1,0,2:T(2,128)S(1)} %get-tuple-element.28), channel_id=1, source_target_pairs={{1,0},{2,1},{3,2},{4,3},{5,4},{6,5},{7,6},{0,7},{9,8},{10,9},{11,1... | collective-permute-start | bytes 33800 | tf_op jit(solution)/shard_map/ppermute | solution.py:22
  103.7 1.4 copy-start.3
  104.0 2.2 copy-start.4
